TPU v7x, 32 devices: a whole 2x2x4 slice. The times are simulated.
32 devices in a mesh: depth: 16 (over z, y, x), spec: 2 (over core).
Axes of the slice: x: 2, y: 2, z: 4, core: 2. Of those that a mesh axis runs over, the one named last changes fastest.
Arguments:
- emission: bfloat16 [512, 64, 2048], P('depth', 'spec'), may hold values from 0.099609375 to 2
- opacity: bfloat16 [512, 64, 2048], P('depth', 'spec'), may hold values from 0.29882812 to 3
- bin_extinction: float32 [64], P('spec'), may hold values from 0.1 to 30
- entry: int32 [2048], replicated, may hold values from 0 to 127
- exit_cell: int32 [2048], replicated, may hold values from 384 to 512
- response: float32 [3, 64], P(None, 'spec'), may hold values from 0.05 to 1
Outputs:
- nearer_slab_rgb: float32 [16, 3, 2048], P('depth')
- image: float32 [3, 2048], replicated
All inputs are finite; a program needn't handle non-finite values.
Results may differ from a plain program's by a relative error of at most 0.0003.
Values sent between devices are 32-bit elements; how exact they have to be, the bound alone decides.
A program may use at most 64 MiB of HBM per device.

v0:
```python
import jax
import jax.numpy as jnp
from jax import lax
from jax.sharding import PartitionSpec as P


def merge_slabs(earlier, later):
    return (earlier[0] + earlier[1] * later[0], earlier[1] * later[1])


def body(emission, opacity, bin_extinction, entry, exit_cell, response):
    cells = emission.shape[0]
    sections = lax.axis_size("depth")
    cell_step = 1.0 / (cells * sections)
    depth = lax.axis_index("depth") * cells + jnp.arange(cells, dtype=jnp.int32)
    inside = (depth[:, None] >= entry[None, :]) & (depth[:, None] < exit_cell[None, :])
    live = jnp.where(inside, 1.0, 0.0).astype(jnp.float32)
    tau = bin_extinction[None, :, None] * opacity.astype(jnp.float32) * live[:, None, :] * cell_step
    rows = jnp.arange(cells, dtype=jnp.int32)
    lower = jnp.where(rows[None, :] < rows[:, None], 1.0, 0.0).astype(jnp.float32)
    before = jnp.einsum("ij,jbr->ibr", lower, tau, precision=lax.Precision.HIGHEST)
    light = jnp.sum(
        emission.astype(jnp.float32) * live[:, None, :] * cell_step * jnp.exp(-before), axis=0
    )
    trans = jnp.exp(-jnp.sum(tau, axis=0))
    pieces = (
        lax.all_to_all(light[None], "depth", split_axis=2, concat_axis=0, tiled=True),
        lax.all_to_all(trans[None], "depth", split_axis=2, concat_axis=0, tiled=True),
    )
    totals = lax.associative_scan(merge_slabs, (pieces[0], pieces[1]), axis=0)
    lead_light = jnp.concatenate([jnp.zeros_like(pieces[0][:1]), totals[0][:-1]], axis=0)
    lead_trans = jnp.concatenate([jnp.ones_like(pieces[1][:1]), totals[1][:-1]], axis=0)
    moved_light = lax.all_to_all(lead_light, "depth", split_axis=0, concat_axis=2, tiled=True)
    moved_trans = lax.all_to_all(lead_trans, "depth", split_axis=0, concat_axis=2, tiled=True)
    nearer_radiance = moved_light[0]
    nearer_transparency = moved_trans[0]
    front_part = jnp.dot(response, nearer_radiance, precision=lax.Precision.HIGHEST)
    slab_portion = jnp.dot(response, nearer_transparency * light, precision=lax.Precision.HIGHEST)
    nearer_slab_rgb, slab_colour_rgb = lax.psum((front_part, slab_portion), "spec")
    image = lax.psum(slab_colour_rgb, "depth")
    return (nearer_slab_rgb[None], image)


def solution(mesh):
    placed = (
        P("depth", "spec", None),
        P("depth", "spec", None),
        P("spec"),
        P(),
        P(),
        P(None, "spec"),
    )
    return jax.shard_map(
        body, mesh=mesh, in_specs=placed, out_specs=(P("depth", None, None), P()), check_vma=False
    )
```

profile of v0, /device:TPU:0, one launch (start us, length us, event | category | flops | bytes accessed | tf_op | source)
XLA Modules:
  0.0 190.8 jit_solution(17573433646198136472)
XLA Ops:
  0.7 0.8 and_select_fusion
  1.5 5.9 %fusion = f32[32,2048]{1,0:T(8,128)S(1)} fusion(f32[32]{0:T(128)} %param.8, f32[32,2048]{1,0:T(8,128)S(1)} %and_select_fusion, bf16[32,32,2048]{2,1,0:T(8,128)(2,1)} %param.7), kind=kLoop, calls=%fused_computation.2 | loop fusion | flops 10420224 | bytes 4718720 | tf_op jit(solution)/shard_map/reduce_sum | solution.py:25
  7.4 0.6 copy.48
  8.0 0.5 broadcast.88
  8.5 9.3 %reduce = f32[2048,32]{1,0:T(8,128)S(1)} reduce(f32[2048,1,32]{2,1,0:T(1,128)S(1)} %bitcast.63, f32[]{:T(128)} %broadcast.88), dimensions={1}, to_apply=%bitcast.47.reduce_sub_computation | reduce | bytes 524292
  17.9 1.1 reshape.76
  19.0 8.3 %all-to-all-start.1 = ((f32[16,1,4096]{2,1,0:T(1,128)}), f32[16,1,4096]{2,1,0:T(1,128)S(1)}, u32[]{:S(2)}, u32[]{:S(2)}) async-start(f32[16,1,4096]{2,1,0:T(1,128)} %reshape.76), calls=%async_computation.1 | async-start | bytes 524288 | tf_op jit(solution)/shard_map/all_to_all | solution.py:28
  27.4 21.2 %multiply_reduce_fusion = f32[32,2048]{1,0:T(8,128)S(1)} fusion(bf16[32,32,2048]{2,1,0:T(8,128)(2,1)} %param.6, f32[32]{0:T(128)S(1)} %copy-done.1, f32[32,2048]{1,0:T(8,128)S(1)} %and_select_fusion, bf16[32,32,2048]{2,1,0:T(8,128)(2,1)} %param.7), kind=kOutput, calls=%fused_computation | convolution fusion | flops 826214400 | bytes 8913024 | tf_op jit(solution)/shard_map/ij,jbr->ibr/dot_general | solution.py:21
  48.6 0.6 copy.46
  49.2 9.6 %reduce.2 = f32[2048,32]{1,0:T(8,128)S(1)} reduce(f32[2048,1,32]{2,1,0:T(1,128)S(1)} %bitcast.66, f32[]{:T(128)} %broadcast.88), dimensions={1}, to_apply=%bitcast.45.reduce_sub_computation | reduce | bytes 524292
  58.8 1.2 reshape.74
  59.9 6.9 %all-to-all-start = ((f32[16,1,4096]{2,1,0:T(1,128)}), f32[16,1,4096]{2,1,0:T(1,128)S(1)}, u32[]{:S(2)}, u32[]{:S(2)}) async-start(f32[16,1,4096]{2,1,0:T(1,128)} %reshape.74), calls=%async_computation | async-start | bytes 524288 | tf_op jit(solution)/shard_map/all_to_all | solution.py:27
  66.8 1.3 reduce.1
  68.1 1.8 reshape.77
  69.9 0.6 copy.49
  70.9 5.3 %all-to-all-done = f32[16,1,4096]{2,1,0:T(1,128)S(1)} async-done(((f32[16,1,4096]{2,1,0:T(1,128)}), f32[16,1,4096]{2,1,0:T(1,128)S(1)}, u32[]{:S(2)}, u32[]{:S(2)}) %all-to-all-start) | async-done | bytes 262176 | tf_op jit(solution)/shard_map/all_to_all | solution.py:27
  76.2 1.3 reduce.3
  77.4 1.8 reshape.75
  79.3 0.3 copy.57
  81.5 0.4 pad.59
  81.9 0.4 pad.58
  82.4 0.4 pad.56
  82.8 0.4 pad.57
  85.2 0.7 concatenate.31.clone
  85.9 3.5 %all-to-all-start.3 = ((f32[16,32,128]{2,1,0:T(8,128)}), f32[16,32,128]{2,1,0:T(8,128)S(1)}, u32[]{:S(2)}, u32[]{:S(2)}) async-start(f32[16,32,128]{2,1,0:T(8,128)} %concatenate.31.clone), calls=%async_computation.3 | async-start | bytes 524288 | tf_op jit(solution)/shard_map/all_to_all | solution.py:34
  90.1 0.7 concatenate.29.clone
  90.8 7.8 %all-to-all-done.3 = f32[16,32,128]{2,1,0:T(8,128)S(1)} async-done(((f32[16,32,128]{2,1,0:T(8,128)}), f32[16,32,128]{2,1,0:T(8,128)S(1)}, u32[]{:S(2)}, u32[]{:S(2)}) %all-to-all-start.3) | async-done | bytes 262176 | tf_op jit(solution)/shard_map/all_to_all | solution.py:34
  98.7 3.5 %all-to-all-start.2 = ((f32[16,32,128]{2,1,0:T(8,128)}), f32[16,32,128]{2,1,0:T(8,128)S(1)}, u32[]{:S(2)}, u32[]{:S(2)}) async-start(f32[16,32,128]{2,1,0:T(8,128)} %concatenate.29.clone), calls=%async_computation.2 | async-start | bytes 524288 | tf_op jit(solution)/shard_map/all_to_all | solution.py:33
  102.4 9.0 %all-to-all-done.2 = f32[16,32,128]{2,1,0:T(8,128)S(1)} async-done(((f32[16,32,128]{2,1,0:T(8,128)}), f32[16,32,128]{2,1,0:T(8,128)S(1)}, u32[]{:S(2)}, u32[]{:S(2)}) %all-to-all-start.2) | async-done | bytes 262176 | tf_op jit(solution)/shard_map/all_to_all | solution.py:33
  112.2 3.6 %all-reduce.18 = (f32[1,3,2048]{2,1,0:T(4,128)S(1)}, f32[3,2048]{1,0:T(4,128)S(1)}) all-reduce(f32[1,3,2048]{2,1,0:T(4,128)S(1)} %convolution_bitcast_fusion.1, f32[3,2048]{1,0:T(4,128)S(1)} %convolution_bitcast_fusion), channel_id=1, replica_groups=mesh['depth'=16,'spec'=2] {'spec'}, use_global_device_ids=true, to_apply=%region_2.3 | all-reduce | flops 12288 | bytes 98304 | tf_op jit(solution)/shard_map/psum | solution.py:39
  115.8 0.6 copy.56
  116.5 74.4 %psum.23 = f32[3,2048]{1,0:T(4,128)} all-reduce(f32[3,2048]{1,0:T(4,128)S(1)} %get-tuple-element.13), channel_id=1, replica_groups=mesh['depth'=16,'spec'=2] {'depth'}, use_global_device_ids=true, to_apply=%region_4.5 | all-reduce | flops 6144 | bytes 49152 | tf_op jit(solution)/shard_map/psum | solution.py:40
  (61 shorter events, 5.5 us)
Async XLA Ops:
  0.6 110.9 %copy-start = (f32[3,32]{1,0:T(4,128)S(1)}, f32[3,32]{1,0:T(4,128)}, u32[]{:S(2)}) copy-start(f32[3,32]{1,0:T(4,128)} %param.11) | copy-start | bytes 1156
  1.5 25.9 %copy-start.1 = (f32[32]{0:T(128)S(1)}, f32[32]{0:T(128)}, u32[]{:S(2)}) copy-start(f32[32]{0:T(128)} %param.8) | copy-start | bytes 388
  19.0 40.9 %all-to-all-start.1 = ((f32[16,1,4096]{2,1,0:T(1,128)}), f32[16,1,4096]{2,1,0:T(1,128)S(1)}, u32[]{:S(2)}, u32[]{:S(2)}) async-start(f32[16,1,4096]{2,1,0:T(1,128)} %reshape.76), calls=%async_computation.1 | async-start | bytes 524288 | tf_op jit(solution)/shard_map/all_to_all | solution.py:28
  59.9 16.2 %all-to-all-start = ((f32[16,1,4096]{2,1,0:T(1,128)}), f32[16,1,4096]{2,1,0:T(1,128)S(1)}, u32[]{:S(2)}, u32[]{:S(2)}) async-start(f32[16,1,4096]{2,1,0:T(1,128)} %reshape.74), calls=%async_computation | async-start | bytes 524288 | tf_op jit(solution)/shard_map/all_to_all | solution.py:27
  85.9 12.8 %all-to-all-start.3 = ((f32[16,32,128]{2,1,0:T(8,128)}), f32[16,32,128]{2,1,0:T(8,128)S(1)}, u32[]{:S(2)}, u32[]{:S(2)}) async-start(f32[16,32,128]{2,1,0:T(8,128)} %concatenate.31.clone), calls=%async_computation.3 | async-start | bytes 524288 | tf_op jit(solution)/shard_map/all_to_all | solution.py:34
  98.7 12.7 %all-to-all-start.2 = ((f32[16,32,128]{2,1,0:T(8,128)}), f32[16,32,128]{2,1,0:T(8,128)S(1)}, u32[]{:S(2)}, u32[]{:S(2)}) async-start(f32[16,32,128]{2,1,0:T(8,128)} %concatenate.29.clone), calls=%async_computation.2 | async-start | bytes 524288 | tf_op jit(solution)/shard_map/all_to_all | solution.py:33
where the time goes:
time: 192 us; the launch traced here: 191 us
  blocking collectives  78 us (41%)
  other arithmetic  28.9 us (15%)
  starting transfers between devices  22.3 us (12%)
  waiting for transfers between devices  22.1 us (12%)
  matrix products  21.8 us (11%)
  local copies, waits for them, and re-layouts  16.5 us (9%)
    psum x1, blocking collectives, body(): image = lax.psum(slab_colour_rgb, 'depth')  74.4 us
    dot_general x1, matrix products, body(): jnp.einsum('ij,jbr->ibr', lower, tau, precision=lax.Precision.HIGHEST)  21.2 us
    unnamed x2, other arithmetic  18.9 us
    all_to_all x1, waiting for transfers between devices, body(): lax.all_to_all(lead_light, 'depth', split_axis=0, concat_axis=2, tiled=True)  8.99 us
    all_to_all x1, starting transfers between devices, body(): lax.all_to_all(trans[None], 'depth', split_axis=2, concat_axis=0, tiled=T...  8.35 us
    all_to_all x1, waiting for transfers between devices, body(): lax.all_to_all(lead_trans, 'depth', split_axis=0, concat_axis=2, tiled=True)  7.84 us
    unnamed x14, local copies, waits for them, and re-layouts  7.74 us
    all_to_all x1, starting transfers between devices, body(): lax.all_to_all(light[None], 'depth', split_axis=2, concat_axis=0, tiled=T...  6.9 us
  transfers between devices with their start and end apart: 4, of which 3 were waited for; matrix products, arithmetic and copies ran while one was open for 20% of the time, Pallas kernels for 0%

commit v1 on v0

v1 whole, which is shorter than its diff:
```python
import functools
import math
import jax
import jax.numpy as jnp
from jax import lax
from jax.experimental import pallas as pl
from jax.experimental.pallas import tpu as pltpu
from jax.sharding import PartitionSpec as P

LANES = 128
MESH = pl.DeviceIdType.MESH


def column(row, eye):
    return jnp.sum(jnp.where(eye, row, 0.0), axis=1, keepdims=True)


def kernel(
    groups, members, specs,
    em_hbm, op_hbm, ext_ref, entry_ref, exit_ref, resp_ref,
    near_ref, image_ref,
    em_v, op_v, s_out, s_in, l_out, l_in, z_in, z_out, c_own, c_sib, t_out, t_in, f_out, f_in,
    em_sem, op_sem, s_send, s_recv, l_send, l_recv, z_send, z_recv,
    c_send, c_recv, t_send, t_recv, f_send, f_recv,
):
    cells, bins, rays = em_hbm.shape
    part = rays // members
    tiles = part // LANES
    sections = groups * members
    cell_step = 1.0 / (cells * sections)
    me = lax.axis_index("depth")
    spec = lax.axis_index("spec")
    zi = me // members
    mi = me % members

    def owner(t):
        return lax.rem(mi + 1 + t, members)

    def rays_of(q):
        return pl.ds(pl.multiple_of(q * part, LANES), part)

    reads = []
    for hbm, vmem, sem in ((op_hbm, op_v, op_sem), (em_hbm, em_v, em_sem)):
        row = []
        for t in range(members):
            copy = pltpu.make_async_copy(hbm.at[:, :, rays_of(owner(t))], vmem.at[t], sem.at[t])
            copy.start()
            row.append(copy)
        reads.append(row)

    def peer_in_group(t):
        return (zi * members + owner(t), spec)

    outer = [(dz, ds) for dz in range(1, groups) for ds in range(specs)]

    def peer_outer(dz, ds):
        return (lax.rem(zi + dz, groups) * members + mi, lax.rem(spec + ds, specs))

    barrier = pltpu.get_barrier_semaphore()
    for t in range(members - 1):
        pl.semaphore_signal(barrier, inc=1, device_id=peer_in_group(t), device_id_type=MESH)
    for dz, ds in outer:
        pl.semaphore_signal(barrier, inc=1, device_id=peer_outer(dz, ds), device_id_type=MESH)
    for ds in range(1, specs):
        pl.semaphore_signal(
            barrier, inc=1, device_id=(me, lax.rem(spec + ds, specs)), device_id_type=MESH
        )

    eye = lax.broadcasted_iota(jnp.int32, (bins, bins), 0) == lax.broadcasted_iota(
        jnp.int32, (bins, bins), 1
    )
    scale = column(ext_ref[...].reshape(1, bins), eye) * (-cell_step * math.log2(math.e))
    scale = jnp.broadcast_to(scale, (bins, LANES))
    first = me * cells

    def bounds(q, j):
        at = pl.ds(pl.multiple_of(q * part + j * LANES, LANES), LANES)
        low = jnp.broadcast_to(entry_ref[at].reshape(1, LANES) - first, (8, LANES))
        high = jnp.broadcast_to(exit_ref[at].reshape(1, LANES) - first, (8, LANES))
        return low, high

    def live_at(i, low, high):
        return jnp.where((low <= i) & (high > i), 1.0, 0.0)

    def masked(x, live):
        return (x.astype(jnp.float32).reshape(bins // 8, 8, LANES) * live[None]).reshape(bins, LANES)

    def at_tile(j):
        return pl.ds(pl.multiple_of(j * LANES, LANES), LANES)

    sends = []
    for t in range(members):
        reads[0][t].wait()
        q = owner(t)

        @pl.loop(0, tiles)
        def _(j):
            low, high = bounds(q, j)
            total = jnp.zeros((bins, LANES), jnp.float32)
            for i in range(cells):
                total = total + masked(op_v[t, i, :, at_tile(j)], live_at(i, low, high))
            s_out[t, :, at_tile(j)] = total * scale

        if t == 0:
            pl.semaphore_wait(barrier, members - 1 + groups * specs - 1)
        if t < members - 1:
            copy = pltpu.make_async_remote_copy(
                s_out.at[t], s_in.at[mi], s_send.at[t], s_recv.at[mi],
                device_id=peer_in_group(t), device_id_type=MESH,
            )
            copy.start()
            sends.append(copy)

    for t in range(members):
        reads[1][t].wait()
        q = owner(t)

        @pl.loop(0, tiles)
        def _(j):
            low, high = bounds(q, j)
            run = jnp.zeros((bins, LANES), jnp.float32)
            glow = jnp.zeros((bins, LANES), jnp.float32)
            for i in range(cells):
                live = live_at(i, low, high)
                glow = glow + masked(em_v[t, i, :, at_tile(j)], live) * jnp.exp2(run)
                run = run + masked(op_v[t, i, :, at_tile(j)], live) * scale
            l_out[t, :, at_tile(j)] = glow * cell_step

        if t < members - 1:
            copy = pltpu.make_async_remote_copy(
                l_out.at[t], l_in.at[mi], l_send.at[t], l_recv.at[mi],
                device_id=peer_in_group(t), device_id_type=MESH,
            )
            copy.start()
            sends.append(copy)

    s_in[mi] = s_out[members - 1]
    l_in[mi] = l_out[members - 1]
    for t in range(members - 1):
        k = owner(t)
        pltpu.make_async_remote_copy(
            s_out.at[t], s_in.at[k], s_send.at[t], s_recv.at[k],
            device_id=peer_in_group(t), device_id_type=MESH,
        ).wait_recv()

    up = (lax.rem(zi + 1, groups) * members + mi, spec)

    def chain_copy(j):
        return pltpu.make_async_remote_copy(
            z_out.at[j], z_in.at[j], z_send.at[j], z_recv.at[j],
            device_id=up, device_id_type=MESH,
        )

    for j in range(tiles):
        lanes = pl.ds(j * LANES, LANES)
        here = s_in[0, :, lanes]
        for k in range(1, members):
            here = here + s_in[k, :, lanes]

        @pl.when(zi == 0)
        def _():
            z_in[j] = jnp.zeros((bins, LANES), jnp.float32)

        @pl.when(zi > 0)
        def _():
            chain_copy(j).wait_recv()

        @pl.when(zi < groups - 1)
        def _():
            z_out[j] = z_in[j] + here
            chain_copy(j).start()

    for t in range(members - 1):
        k = owner(t)
        pltpu.make_async_remote_copy(
            l_out.at[t], l_in.at[k], l_send.at[t], l_recv.at[k],
            device_id=peer_in_group(t), device_id_type=MESH,
        ).wait_recv()

    colours = resp_ref.shape[0]
    weights = [
        jnp.broadcast_to(column(resp_ref[pl.ds(c, 1), :], eye), (bins, LANES)) for c in range(colours)
    ]

    for j in range(tiles):
        lanes = pl.ds(j * LANES, LANES)
        ahead = z_in[j]
        totals = [None] * colours
        for k in range(members):
            seen = jnp.exp2(ahead) * l_in[k, :, lanes]
            for c in range(colours):
                value = jnp.sum(seen * weights[c], axis=0, keepdims=True)
                c_own[k, pl.ds(c, 1), lanes] = value
                totals[c] = value if k == 0 else totals[c] + value
            if k < members - 1:
                ahead = ahead + s_in[k, :, lanes]
        for c in range(colours):
            t_out[pl.ds(c, 1), lanes] = totals[c]

    for n, (dz, ds) in enumerate(outer):
        copy = pltpu.make_async_remote_copy(
            t_out, t_in.at[zi, spec], t_send.at[n], t_recv.at[zi, spec],
            device_id=peer_outer(dz, ds), device_id_type=MESH,
        )
        copy.start()
        sends.append(copy)
    for ds in range(1, specs):
        copy = pltpu.make_async_remote_copy(
            c_own, c_sib.at[spec], c_send.at[ds], c_recv.at[spec],
            device_id=(me, lax.rem(spec + ds, specs)), device_id_type=MESH,
        )
        copy.start()
        sends.append(copy)

    sums = [c_own[k] for k in range(members)]
    for ds in range(1, specs):
        other = lax.rem(spec + ds, specs)
        pltpu.make_async_remote_copy(
            c_own, c_sib.at[other], c_send.at[ds], c_recv.at[other],
            device_id=(me, other), device_id_type=MESH,
        ).wait_recv()
        sums = [sums[k] + c_sib[other, k] for k in range(members)]

    front = jnp.zeros((colours, part), jnp.float32)
    whole = sums[0]
    for k in range(1, members):
        whole = whole + sums[k]
    for n, (dz, ds) in enumerate(outer):
        z = lax.rem(zi + dz, groups)
        other = lax.rem(spec + ds, specs)
        pltpu.make_async_remote_copy(
            t_out, t_in.at[z, other], t_send.at[n], t_recv.at[z, other],
            device_id=peer_outer(dz, ds), device_id_type=MESH,
        ).wait_recv()
        value = t_in[z, other]
        front = front + value * jnp.where(z < zi, 1.0, 0.0)
        whole = whole + value

    for k in range(members):
        f_out[k, 0] = front
        f_out[k, 1] = whole
        if k < members - 1:
            front = front + sums[k]
    for t in range(members - 1):
        k = owner(t)
        copy = pltpu.make_async_remote_copy(
            f_out.at[k], f_in.at[mi], f_send.at[t], f_recv.at[mi],
            device_id=peer_in_group(t), device_id_type=MESH,
        )
        copy.start()
        sends.append(copy)
    near_ref[0, :, rays_of(mi)] = f_out[mi, 0]
    image_ref[:, rays_of(mi)] = f_out[mi, 1]
    for t in range(members - 1):
        k = owner(t)
        pltpu.make_async_remote_copy(
            f_out.at[k], f_in.at[k], f_send.at[t], f_recv.at[k],
            device_id=peer_in_group(t), device_id_type=MESH,
        ).wait_recv()
        near_ref[0, :, rays_of(k)] = f_in[k, 0]
        image_ref[:, rays_of(k)] = f_in[k, 1]

    for copy in sends:
        copy.wait_send()

    @pl.when(zi < groups - 1)
    def _():
        for j in range(tiles):
            chain_copy(j).wait_send()


def body(groups, members, specs, emission, opacity, bin_extinction, entry, exit_cell, response):
    cells, bins, rays = emission.shape
    colours = response.shape[0]
    part = rays // members
    tiles = part // LANES
    f32 = jnp.float32
    vmem = pl.BlockSpec(memory_space=pltpu.VMEM)
    hbm = pl.BlockSpec(memory_space=pltpu.HBM)
    dma = pltpu.SemaphoreType.DMA
    return pl.pallas_call(
        functools.partial(kernel, groups, members, specs),
        out_shape=(
            jax.ShapeDtypeStruct((1, colours, rays), f32),
            jax.ShapeDtypeStruct((colours, rays), f32),
        ),
        in_specs=[hbm, hbm, vmem, vmem, vmem, vmem],
        out_specs=(vmem, vmem),
        scratch_shapes=[
            pltpu.VMEM((members, cells, bins, part), emission.dtype),
            pltpu.VMEM((members, cells, bins, part), opacity.dtype),
            pltpu.VMEM((members, bins, part), f32),
            pltpu.VMEM((members, bins, part), f32),
            pltpu.VMEM((members, bins, part), f32),
            pltpu.VMEM((members, bins, part), f32),
            pltpu.VMEM((tiles, bins, LANES), f32),
            pltpu.VMEM((tiles, bins, LANES), f32),
            pltpu.VMEM((members, colours, part), f32),
            pltpu.VMEM((specs, members, colours, part), f32),
            pltpu.VMEM((colours, part), f32),
            pltpu.VMEM((groups, specs, colours, part), f32),
            pltpu.VMEM((members, 2, colours, part), f32),
            pltpu.VMEM((members, 2, colours, part), f32),
            dma((members,)), dma((members,)),
            dma((members,)), dma((members,)),
            dma((members,)), dma((members,)),
            dma((tiles,)), dma((tiles,)),
            dma((specs,)), dma((specs,)),
            dma((groups * specs,)), dma((groups, specs)),
            dma((members,)), dma((members,)),
        ],
        compiler_params=pltpu.CompilerParams(
            collective_id=0, has_side_effects=True, vmem_limit_bytes=56 * 2**20
        ),
    )(emission, opacity, bin_extinction, entry, exit_cell, response)


def solution(mesh):
    sections = mesh.shape["depth"]
    groups = next(g for g in range(1, sections + 1) if sections % g == 0 and g * g >= sections)
    placed = (
        P("depth", "spec", None),
        P("depth", "spec", None),
        P("spec"),
        P(),
        P(),
        P(None, "spec"),
    )
    return jax.shard_map(
        functools.partial(body, groups, sections // groups, mesh.shape["spec"]),
        mesh=mesh, in_specs=placed, out_specs=(P("depth", None, None), P()), check_vma=False,
    )
```

time: 192 us -> 33 us (0.17)
  blocking collectives: 78 us -> 0 us
  Pallas kernels: 0 us -> 29.3 us
  other arithmetic: 28.9 us -> 0 us
  starting transfers between devices: 22.3 us -> 0 us
  waiting for transfers between devices: 22.1 us -> 0 us
  matrix products: 21.8 us -> 0 us
  local copies, waits for them, and re-layouts: 16.5 us -> 2.77 us
    psum x2 -> x0, blocking collectives: 78 us -> none  [the longest x1 74.4 us: body(): image = lax.psum(slab_colour_rgb, 'depth')]
    pallas_call x0 -> x1, Pallas kernels: none -> 29.3 us  [body(): pl.pallas_call(functools.partial(kernel, groups, members, specs), out_sha...]
    all_to_all x4 -> x0, starting transfers between devices: 22.3 us -> none  [the longest x1 8.35 us: body(): lax.all_to_all(trans[None], 'depth', split_axis=2, concat_axis=0, tiled=T...]
    all_to_all x4 -> x0, waiting for transfers between devices: 22.1 us -> none  [the longest x1 8.99 us: body(): lax.all_to_all(lead_light, 'depth', split_axis=0, concat_axis=2, tiled=True)]
    dot_general x3 -> x0, matrix products: 21.8 us -> none  [the longest x1 21.2 us: body(): jnp.einsum('ij,jbr->ibr', lower, tau, precision=lax.Precision.HIGHEST)]
    unnamed x2 -> x0, other arithmetic: 18.9 us -> none
    unnamed x14 -> x1, local copies, waits for them, and re-layouts: 7.74 us -> 1.38 us
    reduce_sum x1 -> x0, other arithmetic: 5.89 us -> none  [body(): trans = jnp.exp(-jnp.sum(tau, axis=0))]
  transfers between devices with their start and end apart: 4 -> 0, of which waited for: 3 -> 0; matrix products, arithmetic and copies ran while one was open for 20% -> 0% of each run, Pallas kernels for 0% -> 0%
where the time goes in v1:
time: 33 us; the launch traced here: 32.7 us
  Pallas kernels  29.3 us (89%)
  local copies, waits for them, and re-layouts  2.77 us (8%)
  between operations  0.64 us (2%)
    pallas_call x1, Pallas kernels, body(): pl.pallas_call(functools.partial(kernel, groups, members, specs), out_sha...  29.3 us
    pallas_call x1, local copies, waits for them, and re-layouts, body(): pl.pallas_call(functools.partial(kernel, groups, members, specs), out_sha...  1.39 us
    unnamed x1, local copies, waits for them, and re-layouts  1.38 us

profile of v1, /device:TPU:0, one launch (start us, length us, event | category | flops | bytes accessed | tf_op | source)
XLA Modules:
  0.0 32.7 jit_solution(11378622298465726221)
XLA Ops:
  0.6 29.3 %shard_map.77 = (f32[1,3,2048]{2,1,0:T(4,128)}, f32[3,2048]{1,0:T(4,128)}) custom-call(bf16[32,32,2048]{2,1,0:T(8,128)(2,1)} %em_hbm.1, bf16[32,32,2048]{2,1,0:T(8,128)(2,1)} %op_hbm.1, f32[32]{0:T(128)} %ext_ref.1, s32[2048]{0:T(1024)} %entry_ref.1, s32[2048]{0:T(1024)} %exit_ref.1, f32[3,32]{1,0:T(4,128)} %resp_ref.1), custom_call_target="tpu_custom_call" | custom-call | tf_op jit(solution)/shard_map/pallas_call | solution.py:281
  29.9 1.4 %copy.8 = f32[1,3,2048]{2,0,1:T(1,128)} copy(f32[1,3,2048]{2,1,0:T(4,128)} %get-tuple-element.2) | data formatting | bytes 49152 | tf_op jit(solution)/shard_map/pallas_call | solution.py:281
  31.3 1.4 %copy.10 = f32[3,2048]{1,0:T(4,128)} copy(f32[3,2048]{1,0:T(4,128)} %get-tuple-element.7) | data formatting | bytes 49152

commit v2 on v1

--- a/solution.py
+++ b/solution.py
@@ -20,8 +20,9 @@
     em_hbm, op_hbm, ext_ref, entry_ref, exit_ref, resp_ref,
     near_ref, image_ref,
     em_v, op_v, s_out, s_in, l_out, l_in, z_in, z_out, c_own, c_sib, t_out, t_in, f_out, f_in,
+    r_out, r_in, i_out, i_in, front_v, whole_v,
     em_sem, op_sem, s_send, s_recv, l_send, l_recv, z_send, z_recv,
-    c_send, c_recv, t_send, t_recv, f_send, f_recv,
+    c_send, c_recv, t_send, t_recv, f_send, f_recv, r_send, r_recv, i_send, i_recv,
 ):
     cells, bins, rays = em_hbm.shape
     part = rays // members
@@ -143,6 +144,46 @@
             device_id=peer_in_group(t), device_id_type=MESH,
         ).wait_recv()
 
+    half = groups // 2
+
+    def wait_light():
+        for t in range(members - 1):
+            k = owner(t)
+            pltpu.make_async_remote_copy(
+                l_out.at[t], l_in.at[k], l_send.at[t], l_recv.at[k],
+                device_id=peer_in_group(t), device_id_type=MESH,
+            ).wait_recv()
+
+    def group_light(lanes):
+        ahead = s_in[0, :, lanes]
+        light = l_in[0, :, lanes]
+        for k in range(1, members):
+            light = light + jnp.exp2(ahead) * l_in[k, :, lanes]
+            ahead = ahead + s_in[k, :, lanes]
+        return light, ahead
+
+    down = (lax.rem(zi + groups - 1, groups) * members + mi, spec)
+
+    def down_copy(j):
+        return pltpu.make_async_remote_copy(
+            r_out.at[j], r_in.at[j], r_send.at[j], r_recv.at[j],
+            device_id=down, device_id_type=MESH,
+        )
+
+    @pl.when(zi > half)
+    def _():
+        wait_light()
+        for j in range(tiles):
+            light, depth = group_light(pl.ds(j * LANES, LANES))
+            r_out[j] = light
+
+            @pl.when(zi < groups - 1)
+            def _():
+                down_copy(j).wait_recv()
+                r_out[j] = light + jnp.exp2(depth) * r_in[j]
+
+            down_copy(j).start()
+
     up = (lax.rem(zi + 1, groups) * members + mi, spec)
 
     def chain_copy(j):
@@ -170,17 +211,37 @@
             z_out[j] = z_in[j] + here
             chain_copy(j).start()
 
-    for t in range(members - 1):
-        k = owner(t)
-        pltpu.make_async_remote_copy(
-            l_out.at[t], l_in.at[k], l_send.at[t], l_recv.at[k],
-            device_id=peer_in_group(t), device_id_type=MESH,
-        ).wait_recv()
+    @pl.when(zi <= half)
+    def _():
+        wait_light()
 
     colours = resp_ref.shape[0]
     weights = [
         jnp.broadcast_to(column(resp_ref[pl.ds(c, 1), :], eye), (bins, LANES)) for c in range(colours)
     ]
+
+    everyone = [(dz, ds) for dz in range(groups) for ds in range(specs) if dz + ds > 0]
+
+    def image_copy(n, source):
+        return pltpu.make_async_remote_copy(
+            i_out, i_in.at[source], i_send.at[n], i_recv.at[source],
+            device_id=peer_outer(*everyone[n]), device_id_type=MESH,
+        )
+
+    @pl.when(zi == half)
+    def _():
+        for j in range(tiles):
+            lanes = pl.ds(j * LANES, LANES)
+            light, depth = group_light(lanes)
+            if half < groups - 1:
+                down_copy(j).wait_recv()
+                light = light + jnp.exp2(depth) * r_in[j]
+            seen = jnp.exp2(z_in[j]) * light
+            for c in range(colours):
+                i_out[pl.ds(c, 1), lanes] = jnp.sum(seen * weights[c], axis=0, keepdims=True)
+        for n in range(len(everyone)):
+            image_copy(n, spec).start()
+        i_in[spec] = i_out[...]
 
     for j in range(tiles):
         lanes = pl.ds(j * LANES, LANES)
@@ -197,13 +258,20 @@
         for c in range(colours):
             t_out[pl.ds(c, 1), lanes] = totals[c]
 
+    def total_copy(n, z, source):
+        return pltpu.make_async_remote_copy(
+            t_out, t_in.at[z, source], t_send.at[n], t_recv.at[z, source],
+            device_id=peer_outer(*outer[n]), device_id_type=MESH,
+        )
+
+    def needed(origin, reader):
+        return (origin < half) | (reader > origin)
+
     for n, (dz, ds) in enumerate(outer):
-        copy = pltpu.make_async_remote_copy(
-            t_out, t_in.at[zi, spec], t_send.at[n], t_recv.at[zi, spec],
-            device_id=peer_outer(dz, ds), device_id_type=MESH,
-        )
-        copy.start()
-        sends.append(copy)
+        @pl.when(needed(zi, lax.rem(zi + dz, groups)))
+        def _():
+            total_copy(n, zi, spec).start()
+
     for ds in range(1, specs):
         copy = pltpu.make_async_remote_copy(
             c_own, c_sib.at[spec], c_send.at[ds], c_recv.at[spec],
@@ -221,20 +289,30 @@
         ).wait_recv()
         sums = [sums[k] + c_sib[other, k] for k in range(members)]
 
-    front = jnp.zeros((colours, part), jnp.float32)
+    front_v[...] = jnp.zeros((colours, part), jnp.float32)
     whole = sums[0]
     for k in range(1, members):
         whole = whole + sums[k]
+    whole_v[...] = whole * jnp.where(zi < half, 1.0, 0.0)
     for n, (dz, ds) in enumerate(outer):
         z = lax.rem(zi + dz, groups)
         other = lax.rem(spec + ds, specs)
-        pltpu.make_async_remote_copy(
-            t_out, t_in.at[z, other], t_send.at[n], t_recv.at[z, other],
-            device_id=peer_outer(dz, ds), device_id_type=MESH,
-        ).wait_recv()
-        value = t_in[z, other]
-        front = front + value * jnp.where(z < zi, 1.0, 0.0)
-        whole = whole + value
+
+        @pl.when(needed(z, zi))
+        def _():
+            total_copy(n, z, other).wait_recv()
+            value = t_in[z, other]
+            front_v[...] = front_v[...] + value * jnp.where(z < zi, 1.0, 0.0)
+            whole_v[...] = whole_v[...] + value * jnp.where(z < half, 1.0, 0.0)
+
+    front = front_v[...]
+    whole = whole_v[...]
+    for source in range(specs):
+        @pl.when((zi != half) | (spec != source))
+        def _():
+            image_copy(0, source).wait_recv()
+
+        whole = whole + i_in[source]
 
     for k in range(members):
         f_out[k, 0] = front
@@ -263,10 +341,31 @@
     for copy in sends:
         copy.wait_send()
 
+    for n, (dz, ds) in enumerate(outer):
+        @pl.when(needed(zi, lax.rem(zi + dz, groups)))
+        def _():
+            total_copy(n, zi, spec).wait_send()
+
     @pl.when(zi < groups - 1)
     def _():
         for j in range(tiles):
             chain_copy(j).wait_send()
+
+    @pl.when(zi > half)
+    def _():
+        for j in range(tiles):
+            down_copy(j).wait_send()
+
+    @pl.when(zi == half)
+    def _():
+        for n in range(len(everyone)):
+            image_copy(n, spec).wait_send()
+
+
+def place(near_ref, image_ref, near_out, image_out):
+    for c in range(near_out.shape[0]):
+        near_out[c] = near_ref[:, c]
+    image_out[...] = image_ref[...]
 
 
 def body(groups, members, specs, emission, opacity, bin_extinction, entry, exit_cell, response):
@@ -278,7 +377,7 @@
     vmem = pl.BlockSpec(memory_space=pltpu.VMEM)
     hbm = pl.BlockSpec(memory_space=pltpu.HBM)
     dma = pltpu.SemaphoreType.DMA
-    return pl.pallas_call(
+    near, image = pl.pallas_call(
         functools.partial(kernel, groups, members, specs),
         out_shape=(
             jax.ShapeDtypeStruct((1, colours, rays), f32),
@@ -301,6 +400,12 @@
             pltpu.VMEM((groups, specs, colours, part), f32),
             pltpu.VMEM((members, 2, colours, part), f32),
             pltpu.VMEM((members, 2, colours, part), f32),
+            pltpu.VMEM((tiles, bins, LANES), f32),
+            pltpu.VMEM((tiles, bins, LANES), f32),
+            pltpu.VMEM((colours, part), f32),
+            pltpu.VMEM((specs, colours, part), f32),
+            pltpu.VMEM((colours, part), f32),
+            pltpu.VMEM((colours, part), f32),
             dma((members,)), dma((members,)),
             dma((members,)), dma((members,)),
             dma((members,)), dma((members,)),
@@ -308,11 +413,23 @@
             dma((specs,)), dma((specs,)),
             dma((groups * specs,)), dma((groups, specs)),
             dma((members,)), dma((members,)),
+            dma((tiles,)), dma((tiles,)),
+            dma((groups * specs,)), dma((specs,)),
         ],
         compiler_params=pltpu.CompilerParams(
             collective_id=0, has_side_effects=True, vmem_limit_bytes=56 * 2**20
         ),
     )(emission, opacity, bin_extinction, entry, exit_cell, response)
+    near, image = pl.pallas_call(
+        place,
+        out_shape=(
+            jax.ShapeDtypeStruct((colours, 1, rays), f32),
+            jax.ShapeDtypeStruct((colours, rays), f32),
+        ),
+        in_specs=[vmem, vmem],
+        out_specs=(vmem, vmem),
+    )(near, image)
+    return jnp.transpose(near, (1, 0, 2)), image
 
 
 def solution(mesh):

time: 33 us -> 28.6 us (0.87)
  local copies, waits for them, and re-layouts: 2.77 us -> 0 us
  Pallas kernels: 29.3 us -> 27.8 us
    pallas_call x1, Pallas kernels: 29.3 us -> 26.4 us  [body(): pl.pallas_call(functools.partial(kernel, groups, members, specs), out_sha...]
    pallas_call x0 -> x1, Pallas kernels: none -> 1.4 us  [body(): pl.pallas_call(place, out_shape=(jax.ShapeDtypeStruct((colours, 1, rays),...]
    pallas_call x1 -> x0, local copies, waits for them, and re-layouts: 1.39 us -> none  [body(): pl.pallas_call(functools.partial(kernel, groups, members, specs), out_sha...]
    unnamed x1 -> x0, local copies, waits for them, and re-layouts: 1.38 us -> none
where the time goes in v2:
time: 28.6 us; the launch traced here: 28.4 us
  Pallas kernels  27.8 us (97%)
  between operations  0.64 us (2%)
    pallas_call x1, Pallas kernels, body(): pl.pallas_call(functools.partial(kernel, groups, members, specs), out_sha...  26.4 us
    pallas_call x1, Pallas kernels, body(): pl.pallas_call(place, out_shape=(jax.ShapeDtypeStruct((colours, 1, rays),...  1.4 us

profile of v2, /device:TPU:0, one launch (start us, length us, event | category | flops | bytes accessed | tf_op | source)
XLA Modules:
  0.0 28.4 jit_solution(2675326564867511332)
XLA Ops:
  0.6 26.4 %shard_map.77 = (f32[1,3,2048]{2,1,0:T(4,128)}, f32[3,2048]{1,0:T(4,128)}) custom-call(bf16[32,32,2048]{2,1,0:T(8,128)(2,1)} %em_hbm.1, bf16[32,32,2048]{2,1,0:T(8,128)(2,1)} %op_hbm.1, f32[32]{0:T(128)} %ext_ref.1, s32[2048]{0:T(1024)} %entry_ref.1, s32[2048]{0:T(1024)} %exit_ref.1, f32[3,32]{1,0:T(4,128)} %resp_ref.1), custom_call_target="tpu_custom_call" | custom-call | tf_op jit(solution)/shard_map/pallas_call | solution.py:380
  27.0 1.4 %shard_map.78 = (f32[3,1,2048]{2,1,0:T(1,128)}, f32[3,2048]{1,0:T(4,128)}) custom-call(f32[1,3,2048]{2,1,0:T(4,128)} %get-tuple-element.6.near_ref, f32[3,2048]{1,0:T(4,128)} %get-tuple-element.7.image_ref), custom_call_target="tpu_custom_call" | custom-call | tf_op jit(solution)/shard_map/pallas_call | solution.py:423
